TPU v7x, 32 devices: a whole 2x2x4 slice. The times are simulated.
32 devices in a mesh: dp: 8 (over y, x, core), mp: 4 (over z).
Axes of the slice: x: 2, y: 2, z: 4, core: 2. Of those that a mesh axis runs over, the one named last changes fastest.
Arguments:
- inputs: bfloat16 [1024, 6144], P('dp'), may hold values from -6 to 6
- pre_act: bfloat16 [1024, 12288], P('dp', 'mp'), may hold values from -6 to 6
- out_grad: bfloat16 [1024, 6144], P('dp'), may hold values from -6 to 6
- w_in: bfloat16 [6144, 12288], P(None, 'mp'), may hold values from -0.109375 to 0.109375
- w_out: bfloat16 [12288, 6144], P('mp'), may hold values from -0.0546875 to 0.0546875
- master_in: float32 [6144, 12288], P('dp', 'mp'), may hold values from -0.3 to 0.3
- master_out: float32 [12288, 6144], P('mp', 'dp'), may hold values from -0.3 to 0.3
- row_in: float32 [6144], P('dp'), may hold values from 12.8 to 686.08
- col_in: float32 [12288], P('mp'), may hold values from 25 to 128
- row_out: float32 [12288], P('mp'), may hold values from 25.6 to 1372.16
- col_out: float32 [6144], P('dp'), may hold values from 51 to 256
Outputs:
- input_grad: bfloat16 [1024, 6144], P('dp', 'mp')
- new_master_in: float32 [6144, 12288], P('dp', 'mp')
- new_master_out: float32 [12288, 6144], P('mp', 'dp')
All inputs are finite; a program needn't handle non-finite values.
Results may differ from a plain program's by a relative error of at most 0.012.
Values may be sent and summed in bfloat16 or wider, within the bound.
A program may use at most 256 MiB of HBM per device.

v0:
```python
import math
import jax
import jax.numpy as jnp
from jax import lax
from jax.experimental.layout import Layout, with_layout_constraint
from jax.sharding import PartitionSpec as P

D = 6144
FF = 12288
decay_rate = 0.8
step_size = 0.05
tiny_square = 1e-30


def gelu_parts(pre):
    cumulative = 0.5 * (1.0 + jax.scipy.special.erf(pre * (1.0 / math.sqrt(2.0))))
    density = jnp.exp(-0.5 * pre * pre) * (1.0 / math.sqrt(2.0 * math.pi))
    return (pre * cumulative, cumulative + pre * density)


def contract_rows(left, right):
    return lax.dot_general(
        left, right, (((0,), (0,)), ((), ())), preferred_element_type=jnp.float32
    )


def scatter_pieces(partial, axis):
    size = lax.axis_size(axis)
    me = lax.axis_index(axis)
    width = partial.shape[1] // size
    piece = lambda k: lax.dynamic_slice_in_dim(partial, k * width, width, 1)
    pieces = [piece(me)]
    for shift in range(1, size):
        moved = piece(lax.rem(me + shift, size)).astype(jnp.bfloat16)
        pieces.append(lax.ppermute(moved, axis, [(i, (i + shift) % size) for i in range(size)]))
    return pieces


def body(
    inputs, pre_act, out_grad, w_in, w_out, master_in, master_out, row_in, col_in, row_out, col_out
):
    active, slope = gelu_parts(pre_act.astype(jnp.float32))
    hidden = active.astype(jnp.bfloat16)
    hidden_all = lax.all_gather(hidden, "dp", axis=0, tiled=True)
    out_grad, _ = lax.optimization_barrier((out_grad, hidden))
    out_cols = lax.all_to_all(out_grad, "dp", 1, 0, tiled=True)
    hid_grad = lax.dot_general(
        out_grad, w_out, (((1,), (1,)), ((), ())), preferred_element_type=jnp.float32
    )
    pre_grad = (hid_grad * slope).astype(jnp.bfloat16)
    pre_grad_all = lax.all_gather(pre_grad, "dp", axis=0, tiled=True)
    input_part = lax.dot_general(
        pre_grad, w_in, (((1,), (1,)), ((), ())), preferred_element_type=jnp.float32
    )
    inputs, input_part = lax.optimization_barrier((inputs, input_part))
    in_cols = lax.all_to_all(inputs, "dp", 1, 0, tiled=True)
    pieces = scatter_pieces(input_part, "mp")
    grad_out = contract_rows(hidden_all, out_cols)
    square_out = grad_out * grad_out + tiny_square
    width_out, row_out_sum = lax.psum((jnp.sum(square_out, axis=0), jnp.sum(row_out)), "mp")
    cols_out = decay_rate * col_out + (1.0 - decay_rate) * width_out / FF
    hidden_out, sum_out = lax.psum((jnp.sum(square_out, axis=1), jnp.sum(width_out)), "dp")
    rows_out = decay_rate * row_out + (1.0 - decay_rate) * hidden_out / D
    mean_out = (decay_rate * row_out_sum + (1.0 - decay_rate) * sum_out / D) / FF
    update_out = grad_out / jnp.sqrt(rows_out[:, None] * cols_out[None, :] / mean_out)
    new_master_out = master_out - step_size * update_out
    pre_grad_all, new_master_out, pieces = lax.optimization_barrier(
        (pre_grad_all, new_master_out, pieces)
    )
    input_grad = sum((piece.astype(jnp.float32) for piece in pieces)).astype(jnp.bfloat16)
    grad_in = with_layout_constraint(contract_rows(in_cols, pre_grad_all), Layout((0, 1)))
    square_in = grad_in * grad_in + tiny_square
    width_in = lax.psum(jnp.sum(square_in, axis=1), "mp")
    rows_in = decay_rate * row_in + (1.0 - decay_rate) * width_in / FF
    hidden_in, sum_in = lax.psum((jnp.sum(square_in, axis=0), jnp.sum(rows_in)), "dp")
    cols_in = decay_rate * col_in + (1.0 - decay_rate) * hidden_in / D
    mean_in = sum_in / D
    update_in = grad_in / jnp.sqrt(rows_in[:, None] * cols_in[None, :] / mean_in)
    new_master_in = master_in - step_size * update_in
    return (input_grad, new_master_in, new_master_out)


def solution(mesh):
    in_specs = (
        P("dp", None),
        P("dp", "mp"),
        P("dp", None),
        P(None, "mp"),
        P("mp", None),
        P("dp", "mp"),
        P("mp", "dp"),
        P("dp"),
        P("mp"),
        P("mp"),
        P("dp"),
    )
    out_specs = (P("dp", "mp"), P("dp", "mp"), P("mp", "dp"))
    return jax.shard_map(body, mesh=mesh, in_specs=in_specs, out_specs=out_specs, check_vma=False)
```

profile of v0, /device:TPU:0, one launch (start us, length us, event | category | flops | bytes accessed | tf_op | source)
XLA Modules:
  0.0 233.9 jit_solution(13261236055143968567)
XLA Ops:
  7.2 0.0 all-gather.5.cloned.1.call-start
  7.2 2.4 %fusion.8 = bf16[128,3072]{1,0:T(8,128)(2,1)} fusion(bf16[128,3072]{1,0:T(8,128)(2,1)} %param.12), kind=kLoop, calls=%fused_computation.18 | loop fusion | flops 2359296 | bytes 1572864 | tf_op jit(solution)/shard_map/convert_element_type | solution.py:43
  9.6 0.0 all-gather.5.cloned.1.call-update
  9.6 0.0 copy-start.1
  9.6 0.0 all-gather.3.cloned.1.call-start
  9.7 22.5 %fusion.4 = bf16[128,3072]{1,0:T(8,128)(2,1)} fusion(bf16[128,6144]{1,0:T(8,128)(2,1)} %param.13, bf16[3072,6144]{1,0:T(8,128)(2,1)} %param.15, bf16[128,3072]{1,0:T(8,128)(2,1)} %param.12), kind=kOutput, calls=%fused_computation.9 | convolution fusion | flops 4836163584 | bytes 40894464 | tf_op jit(solution)/shard_map/dot_general | solution.py:47
  32.2 0.0 all-gather.3.cloned.1.call-update
  32.2 0.0 copy-done.1
  32.2 1.6 copy.14
  33.8 5.2 %all-to-all-start = ((bf16[128,8,768]{0,2,1:T(8,128)(2,1)}), bf16[128,8,768]{0,2,1:T(8,128)(2,1)}, u32[]{:S(2)}, u32[]{:S(2)}) async-start(bf16[128,8,768]{0,2,1:T(8,128)(2,1)} %bitcast), calls=%async_computation | async-start | bytes 3145728 | tf_op jit(solution)/shard_map/all_to_all | solution.py:46
  39.0 17.9 %fusion.13 = f32[128,6144]{1,0:T(8,128)S(1)} fusion(bf16[128,3072]{1,0:T(8,128)(2,1)} %fusion.4, bf16[6144,3072]{1,0:T(8,128)(2,1)} %param.14), kind=kOutput, calls=%fused_computation.32 | convolution fusion | flops 4831838208 | bytes 41680896 | tf_op jit(solution)/shard_map/dot_general | solution.py:52
  56.9 0.0 copy-start.2
  57.0 2.6 %copy.16 = bf16[128,6144]{0,1:T(8,128)(2,1)} copy(bf16[128,6144]{1,0:T(8,128)(2,1)} %param.11) | data formatting | bytes 3145728 | tf_op jit(solution)/shard_map/optimization_barrier | solution.py:55
  59.5 14.5 %all-to-all-done = bf16[128,8,768]{0,2,1:T(8,128)(2,1)} async-done(((bf16[128,8,768]{0,2,1:T(8,128)(2,1)}), bf16[128,8,768]{0,2,1:T(8,128)(2,1)}, u32[]{:S(2)}, u32[]{:S(2)}) %all-to-all-start) | async-done | bytes 1572896 | tf_op jit(solution)/shard_map/all_to_all | solution.py:46
  74.1 4.3 %all-to-all-start.1 = ((bf16[128,8,768]{0,2,1:T(8,128)(2,1)}), bf16[128,8,768]{0,2,1:T(8,128)(2,1)}, u32[]{:S(2)}, u32[]{:S(2)}) async-start(bf16[128,8,768]{0,2,1:T(8,128)(2,1)} %bitcast.14), calls=%async_computation.1 | async-start | bytes 3145728 | tf_op jit(solution)/shard_map/all_to_all | solution.py:56
  78.4 1.1 dynamic-slice_convert_fusion
  79.4 3.3 %collective-permute-start.2 = (bf16[128,1536]{1,0:T(8,128)(2,1)}, bf16[128,1536]{1,0:T(8,128)(2,1)S(1)}, u32[]{:S(2)}, u32[]{:S(2)}) collective-permute-start(bf16[128,1536]{1,0:T(8,128)(2,1)} %get-tuple-element.33), channel_id=1, source_target_pairs={{0,3},{1,0},{2,1},{3,2},{4,7},{5,4},{6,5},{7,6},{8,11},{9,8},{10,9... | collective-permute-start | bytes 1179656 | tf_op jit(solution)/shard_map/ppermute | solution.py:35
  82.8 0.0 collective-permute-start.1
  82.8 1.1 collective-permute-start
  83.9 0.0 copy-done.2
  83.9 0.6 reduce_sum.65
  84.5 1.0 constant_dynamic-slice_fusion
  85.4 2.6 %copy.15 = bf16[8,128,768]{2,1,0:T(8,128)(2,1)} copy(bf16[8,128,768]{1,2,0:T(8,128)(2,1)} %bitcast.1) | data formatting | bytes 3145728 | tf_op jit(solution)/shard_map/all_to_all | solution.py:46
  88.0 19.7 %all-to-all-done.1 = bf16[128,8,768]{0,2,1:T(8,128)(2,1)} async-done(((bf16[128,8,768]{0,2,1:T(8,128)(2,1)}), bf16[128,8,768]{0,2,1:T(8,128)(2,1)}, u32[]{:S(2)}, u32[]{:S(2)}) %all-to-all-start.1) | async-done | bytes 1572896 | tf_op jit(solution)/shard_map/all_to_all | solution.py:56
  107.7 1.7 copy.17
  109.5 0.0 all-gather.5.cloned.1.call-done
  109.5 0.0 copy-start.4
  109.5 10.4 %fusion.1 = (f32[3072]{0:T(1024)S(1)}, f32[768]{0:T(1024)S(1)}, f32[3072,768]{1,0:T(8,128)}) fusion(bf16[1024,3072]{1,0:T(8,128)(2,1)} %all-gather.5.cloned.1.call-done, bf16[1024,768]{1,0:T(8,128)(2,1)} %bitcast.16), kind=kOutput, calls=%fused_computation.5 | convolution fusion | flops 4841271296 | bytes 17316864 | tf_op jit(solution)/shard_map/dot_general | solution.py:22
  119.9 12.4 %all-reduce.2 = (f32[]{:T(128)}, f32[768]{0:T(1024)S(1)}) all-reduce(f32[]{:T(128)} %reduce_sum.65, f32[768]{0:T(1024)S(1)} %get-tuple-element.24), channel_id=1, replica_groups=mesh['dp'=8,'mp'=4] {'mp'}, use_global_device_ids=true, to_apply=%region_5.0 | all-reduce | flops 769 | bytes 6152 | tf_op jit(solution)/shard_map/psum | solution.py:60
  132.4 0.0 copy-done.4
  132.4 0.6 multiply_add_fusion.5
  133.0 23.4 %all-reduce.1 = (f32[]{:T(128)}, f32[3072]{0:T(1024)S(1)}) all-reduce(f32[]{:T(128)} %get-tuple-element.37, f32[3072]{0:T(1024)S(1)} %get-tuple-element.23), channel_id=1, replica_groups=mesh['dp'=8,'mp'=4] {'dp'}, use_global_device_ids=true, to_apply=%region_7.0 | all-reduce | flops 3073 | bytes 24584 | tf_op jit(solution)/shard_map/psum | solution.py:62
  157.7 11.2 %multiply_subtract_fusion.1 = f32[3072,768]{1,0:T(8,128)} fusion(f32[3072,768]{1,0:T(8,128)} %param.17, f32[3072,768]{1,0:T(8,128)} %get-tuple-element.38, f32[]{:T(128)S(6)} %div.48, f32[768]{0:T(1024)S(1)} %get-tuple-element.36, f32[3072]{0:T(1024)S(1)} %multiply_add_fusion.3), kind=kLoop, calls=%fused_computation.2 | loop fusion | flops 11796480 | bytes 28326916 | tf_op jit(solution)/shard_map/sub | solution.py:66
  169.0 0.0 collective-permute-done.2
  169.0 0.0 collective-permute-done.1
  169.0 0.0 collective-permute-done
  169.0 0.0 all-gather.3.cloned.1.call-done
  169.0 0.0 copy-start.5
  169.0 0.0 copy-start.3
  169.0 0.0 copy-start
  169.0 11.3 %fusion.2 = (f32[3072]{0:T(1024)S(1)}, f32[768]{0:T(1024)S(1)}, f32[768,3072]{1,0:T(8,128)}) fusion(bf16[1024,768]{1,0:T(8,128)(2,1)S(1)} %bitcast.15, bf16[1024,3072]{1,0:T(8,128)(2,1)} %all-gather.3.cloned.1.call-done), kind=kOutput, calls=%fused_computation.6 | convolution fusion | flops 4841271296 | bytes 17316864 | tf_op jit(solution)/shard_map/dot_general | solution.py:22
  180.3 8.3 %psum.53 = f32[768]{0:T(1024)S(1)} all-reduce(f32[768]{0:T(1024)S(1)} %get-tuple-element.22), channel_id=1, replica_groups=mesh['dp'=8,'mp'=4] {'mp'}, use_global_device_ids=true, to_apply=%region_9.0 | all-reduce | flops 768 | bytes 6144 | tf_op jit(solution)/shard_map/psum | solution.py:73
  188.6 0.0 copy-done.5
  188.6 0.6 fusion.12
  189.2 23.4 %all-reduce = (f32[]{:T(128)}, f32[3072]{0:T(1024)S(1)}) all-reduce(f32[]{:T(128)} %get-tuple-element.31, f32[3072]{0:T(1024)S(1)} %get-tuple-element.21), channel_id=1, replica_groups=mesh['dp'=8,'mp'=4] {'dp'}, use_global_device_ids=true, to_apply=%region_13.0 | all-reduce | flops 3073 | bytes 24584 | tf_op jit(solution)/shard_map/psum | solution.py:75
  213.3 0.0 copy-done.3
  213.3 2.0 add_convert_fusion
  215.3 11.7 %multiply_subtract_fusion = f32[768,3072]{1,0:T(8,128)} fusion(f32[768,3072]{1,0:T(8,128)} %param.16, f32[768,3072]{1,0:T(8,128)} %get-tuple-element.39, f32[]{:T(128)S(6)} %div.54, f32[3072]{0:T(1024)S(1)} %multiply_add_fusion.2, f32[768]{0:T(1024)S(1)} %get-tuple-element.32), kind=kLoop, calls=%fused_computation | loop fusion | flops 11796480 | bytes 28326916 | tf_op jit(solution)/shard_map/sub | solution.py:79
  (3 shorter events, 0.0 us)
Async XLA Ops:
  7.2 102.3 %all-gather.5.cloned.1.call-start = ((), (), s32[]{:S(2)}) async-start(), calls=%async_computation.3 | async-start | bytes 7077888 | tf_op jit(solution)/shard_map/all_gather | solution.py:44
  9.6 22.6 %copy-start.1 = (bf16[128,6144]{1,0:T(8,128)(2,1)S(1)}, bf16[128,6144]{1,0:T(8,128)(2,1)}, u32[]{:S(2)}) copy-start(bf16[128,6144]{1,0:T(8,128)(2,1)} %param.13) | copy-start | bytes 4718596
  9.6 159.4 %all-gather.3.cloned.1.call-start = ((), (), s32[]{:S(2)}) async-start(), calls=%async_computation.2 | async-start | bytes 7077888 | tf_op jit(solution)/shard_map/all_gather | solution.py:51
  33.8 40.2 %all-to-all-start = ((bf16[128,8,768]{0,2,1:T(8,128)(2,1)}), bf16[128,8,768]{0,2,1:T(8,128)(2,1)}, u32[]{:S(2)}, u32[]{:S(2)}) async-start(bf16[128,8,768]{0,2,1:T(8,128)(2,1)} %bitcast), calls=%async_computation | async-start | bytes 3145728 | tf_op jit(solution)/shard_map/all_to_all | solution.py:46
  56.9 26.9 %copy-start.2 = (f32[3072]{0:T(1024)S(1)}, f32[3072]{0:T(1024)}, u32[]{:S(2)}) copy-start(f32[3072]{0:T(1024)} %param.20) | copy-start | bytes 36868
  74.1 33.7 %all-to-all-start.1 = ((bf16[128,8,768]{0,2,1:T(8,128)(2,1)}), bf16[128,8,768]{0,2,1:T(8,128)(2,1)}, u32[]{:S(2)}, u32[]{:S(2)}) async-start(bf16[128,8,768]{0,2,1:T(8,128)(2,1)} %bitcast.14), calls=%async_computation.1 | async-start | bytes 3145728 | tf_op jit(solution)/shard_map/all_to_all | solution.py:56
  79.4 89.5 %collective-permute-start.2 = (bf16[128,1536]{1,0:T(8,128)(2,1)}, bf16[128,1536]{1,0:T(8,128)(2,1)S(1)}, u32[]{:S(2)}, u32[]{:S(2)}) collective-permute-start(bf16[128,1536]{1,0:T(8,128)(2,1)} %get-tuple-element.33), channel_id=1, source_target_pairs={{0,3},{1,0},{2,1},{3,2},{4,7},{5,4},{6,5},{7,6},{8,11},{9,8},{10,9... | collective-permute-start | bytes 1179656 | tf_op jit(solution)/shard_map/ppermute | solution.py:35
  82.8 86.2 %collective-permute-start.1 = (bf16[128,1536]{1,0:T(8,128)(2,1)}, bf16[128,1536]{1,0:T(8,128)(2,1)}, u32[]{:S(2)}, u32[]{:S(2)}) collective-permute-start(bf16[128,1536]{1,0:T(8,128)(2,1)} %get-tuple-element.34), channel_id=1, source_target_pairs={{0,2},{1,3},{2,0},{3,1},{4,6},{5,7},{6,4},{7,5},{8,10},{9,11},{10,... | collective-permute-start | bytes 1179656 | tf_op jit(solution)/shard_map/ppermute | solution.py:35
  82.8 86.2 %collective-permute-start = (bf16[128,1536]{1,0:T(8,128)(2,1)}, bf16[128,1536]{1,0:T(8,128)(2,1)}, u32[]{:S(2)}, u32[]{:S(2)}) collective-permute-start(bf16[128,1536]{1,0:T(8,128)(2,1)} %get-tuple-element.35), channel_id=1, source_target_pairs={{0,1},{1,2},{2,3},{3,0},{4,5},{5,6},{6,7},{7,4},{8,9},{9,10},{10,1... | collective-permute-start | bytes 1179656 | tf_op jit(solution)/shard_map/ppermute | solution.py:35
  109.5 22.9 %copy-start.4 = (f32[768]{0:T(1024)S(1)}, f32[768]{0:T(1024)}, u32[]{:S(2)}) copy-start(f32[768]{0:T(1024)} %param.21) | copy-start | bytes 9220
  169.0 19.6 %copy-start.5 = (f32[768]{0:T(1024)S(1)}, f32[768]{0:T(1024)}, u32[]{:S(2)}) copy-start(f32[768]{0:T(1024)} %param.18) | copy-start | bytes 9220
  169.0 44.2 %copy-start.3 = (f32[3072]{0:T(1024)S(1)}, f32[3072]{0:T(1024)}, u32[]{:S(2)}) copy-start(f32[3072]{0:T(1024)} %param.19) | copy-start | bytes 36868
  169.0 44.2 %copy-start = (f32[128,1536]{1,0:T(8,128)S(1)}, f32[128,1536]{1,0:T(8,128)}, u32[]{:S(2)}) copy-start(f32[128,1536]{1,0:T(8,128)} %constant_dynamic-slice_fusion) | copy-start | bytes 2359300
Sparse Core Ops, SparseCore 0:
  9.9 61.8 all-gather.4
  73.7 59.2 all-gather.2
where the time goes:
time: 234 us
  blocking collectives  67.5 us (29%)
  matrix products  62.1 us (27%)
  waiting for transfers between devices  34.3 us (15%)
  other arithmetic  29.2 us (12%)
  between operations  16.2 us (7%)
  starting transfers between devices  14 us (6%)
  local copies, waits for them, and re-layouts  10.5 us (4%)
    psum x1, blocking collectives, body(): lax.psum((jnp.sum(square_out, axis=1), jnp.sum(width_out)), 'dp')  23.4 us
    psum x1, blocking collectives, body(): lax.psum((jnp.sum(square_in, axis=0), jnp.sum(rows_in)), 'dp')  23.4 us
    dot_general x1, matrix products, body(): lax.dot_general(out_grad, w_out, (((1,), (1,)), ((), ())), preferred_elem...  22.5 us
    dot_general x2, matrix products, contract_rows(): lax.dot_general(left, right, (((0,), (0,)), ((), ())), preferred_element_...  21.7 us
    all_to_all x1, waiting for transfers between devices, body(): in_cols = lax.all_to_all(inputs, 'dp', 1, 0, tiled=True)  19.7 us
    dot_general x1, matrix products, body(): lax.dot_general(pre_grad, w_in, (((1,), (1,)), ((), ())), preferred_eleme...  17.9 us
    all_to_all x1, waiting for transfers between devices, body(): out_cols = lax.all_to_all(out_grad, 'dp', 1, 0, tiled=True)  14.5 us
    psum x1, blocking collectives, body(): lax.psum((jnp.sum(square_out, axis=0), jnp.sum(row_out)), 'mp')  12.4 us
  transfers between devices with their start and end apart: 7, of which 2 were waited for; matrix products, arithmetic and copies ran while one was open for 32% of the time, Pallas kernels for 0%

commit v1 on v0

--- a/solution.py
+++ b/solution.py
@@ -53,7 +53,10 @@
         pre_grad, w_in, (((1,), (1,)), ((), ())), preferred_element_type=jnp.float32
     )
     inputs, input_part = lax.optimization_barrier((inputs, input_part))
-    in_cols = lax.all_to_all(inputs, "dp", 1, 0, tiled=True)
+    in_cols = jnp.concatenate(
+        lax.all_to_all(jnp.stack(jnp.split(inputs, lax.axis_size("dp"), axis=1)), "dp", 0, 0),
+        axis=0,
+    )
     pieces = scatter_pieces(input_part, "mp")
     grad_out = contract_rows(hidden_all, out_cols)
     square_out = grad_out * grad_out + tiny_square

time: 234 us -> 208 us (0.89)
  waiting for transfers between devices: 34.3 us -> 0.07 us
  local copies, waits for them, and re-layouts: 10.5 us -> 19.2 us
    all_to_all x1, waiting for transfers between devices: 19.7 us -> 0.01 us  [body(): lax.all_to_all(jnp.stack(jnp.split(inputs, lax.axis_size('dp'), axis=1)),...]
    all_to_all x1, waiting for transfers between devices: 14.5 us -> 0.01 us  [body(): out_cols = lax.all_to_all(out_grad, 'dp', 1, 0, tiled=True)]
    unnamed x12 -> x21, local copies, waits for them, and re-layouts: 0.04 us -> 11.4 us
    dot_general x1, matrix products: 22.5 us -> 19.9 us  [body(): lax.dot_general(out_grad, w_out, (((1,), (1,)), ((), ())), preferred_elem...]
    optimization_barrier x1 -> x0, local copies, waits for them, and re-layouts: 2.58 us -> none  [body(): inputs, input_part = lax.optimization_barrier((inputs, input_part))]
  transfers between devices with their start and end apart: 7 -> 7, of which waited for: 2 -> 0; matrix products, arithmetic and copies ran while one was open for 32% -> 39% of each run, Pallas kernels for 0% -> 0%
where the time goes in v1:
time: 208 us
  blocking collectives  68.1 us (33%)
  matrix products  61 us (29%)
  other arithmetic  29.5 us (14%)
  local copies, waits for them, and re-layouts  19.2 us (9%)
  between operations  16 us (8%)
  starting transfers between devices  13.8 us (7%)
    psum x1, blocking collectives, body(): lax.psum((jnp.sum(square_out, axis=1), jnp.sum(width_out)), 'dp')  25 us
    psum x1, blocking collectives, body(): lax.psum((jnp.sum(square_in, axis=0), jnp.sum(rows_in)), 'dp')  23.4 us
    dot_general x2, matrix products, contract_rows(): lax.dot_general(left, right, (((0,), (0,)), ((), ())), preferred_element_...  22.1 us
    dot_general x1, matrix products, body(): lax.dot_general(out_grad, w_out, (((1,), (1,)), ((), ())), preferred_elem...  19.9 us
    dot_general x1, matrix products, body(): lax.dot_general(pre_grad, w_in, (((1,), (1,)), ((), ())), preferred_eleme...  19 us
    sub x1, other arithmetic, body(): new_master_in = master_in - step_size * update_in  11.7 us
    unnamed x21, local copies, waits for them, and re-layouts  11.4 us
    psum x1, blocking collectives, body(): lax.psum((jnp.sum(square_out, axis=0), jnp.sum(row_out)), 'mp')  11.4 us
  transfers between devices with their start and end apart: 7, of which 0 were waited for; matrix products, arithmetic and copies ran while one was open for 39% of the time, Pallas kernels for 0%

profile of v1, /device:TPU:0, one launch (start us, length us, event | category | flops | bytes accessed | tf_op | source)
XLA Modules:
  0.0 207.8 jit_solution(2293769981630615319)
XLA Ops:
  7.2 0.0 all-gather.5.cloned.1.call-start
  7.2 2.5 %fusion.8 = bf16[128,3072]{1,0:T(8,128)(2,1)} fusion(bf16[128,3072]{1,0:T(8,128)(2,1)} %param.12), kind=kLoop, calls=%fused_computation.18 | loop fusion | flops 2359296 | bytes 1572864 | tf_op jit(solution)/shard_map/convert_element_type | solution.py:43
  9.7 0.0 all-gather.5.cloned.1.call-update
  9.8 0.0 all-gather.3.cloned.1.call-start
  9.8 0.0 copy-done.2
  9.8 0.0 copy-done.1
  9.8 19.9 %fusion.4 = bf16[128,3072]{1,0:T(8,128)(2,1)} fusion(bf16[128,6144]{1,0:T(8,128)(2,1)S(1)} %copy-done.1, bf16[3072,6144]{1,0:T(8,128)(2,1)} %param.15, bf16[128,3072]{1,0:T(8,128)(2,1)S(1)} %copy-done.2), kind=kOutput, calls=%fused_computation.9 | convolution fusion | flops 4836163584 | bytes 40894464 | tf_op jit(solution)/shard_map/dot_general | solution.py:47
  29.8 0.0 all-gather.3.cloned.1.call-update
  29.8 1.6 copy.14
  31.4 4.9 %all-to-all-start = ((bf16[128,8,768]{0,2,1:T(8,128)(2,1)}), bf16[128,8,768]{0,2,1:T(8,128)(2,1)}, u32[]{:S(2)}, u32[]{:S(2)}) async-start(bf16[128,8,768]{0,2,1:T(8,128)(2,1)} %bitcast), calls=%async_computation | async-start | bytes 3145728 | tf_op jit(solution)/shard_map/all_to_all | solution.py:46
  36.3 19.0 %fusion.13 = f32[128,6144]{1,0:T(8,128)S(1)} fusion(bf16[128,3072]{1,0:T(8,128)(2,1)} %fusion.4, bf16[6144,3072]{1,0:T(8,128)(2,1)} %param.14), kind=kOutput, calls=%fused_computation.40 | convolution fusion | flops 4831838208 | bytes 41680896 | tf_op jit(solution)/shard_map/dot_general | solution.py:52
  55.2 0.0 copy-start.3
  55.3 1.1 dynamic-slice_convert_fusion
  56.3 4.0 %collective-permute-start.2 = (bf16[128,1536]{1,0:T(8,128)(2,1)}, bf16[128,1536]{1,0:T(8,128)(2,1)S(1)}, u32[]{:S(2)}, u32[]{:S(2)}) collective-permute-start(bf16[128,1536]{1,0:T(8,128)(2,1)} %get-tuple-element.33), channel_id=1, source_target_pairs={{0,3},{1,0},{2,1},{3,2},{4,7},{5,4},{6,5},{7,6},{8,11},{9,8},{10,9... | collective-permute-start | bytes 1179656 | tf_op jit(solution)/shard_map/ppermute | solution.py:35
  60.3 0.0 collective-permute-start.1
  60.3 1.1 collective-permute-start
  61.4 0.0 copy-done.3
  61.4 0.6 reduce_sum.65
  62.0 1.6 bitcast_dynamic-update-slice_fusion.7
  63.6 1.6 bitcast_dynamic-update-slice_fusion.6
  65.2 1.7 bitcast_dynamic-update-slice_fusion.5
  66.9 1.6 bitcast_dynamic-update-slice_fusion.4
  68.5 1.6 bitcast_dynamic-update-slice_fusion.3
  70.2 1.6 bitcast_dynamic-update-slice_fusion.2
  71.8 1.6 bitcast_dynamic-update-slice_fusion.1
  73.4 1.6 bitcast_dynamic-update-slice_fusion
  75.0 1.0 constant_dynamic-slice_fusion
  76.0 0.0 all-to-all-done
  76.0 3.8 %all-to-all-start.1 = ((bf16[8,128,768]{2,1,0:T(8,128)(2,1)}), bf16[8,128,768]{2,1,0:T(8,128)(2,1)S(1)}, u32[]{:S(2)}, u32[]{:S(2)}) async-start(bf16[8,128,768]{2,1,0:T(8,128)(2,1)} %bitcast_dynamic-update-slice_fusion), calls=%async_computation.1 | async-start | bytes 3145728 | tf_op jit(solution)/shard_map/all_to_all | solution.py:57
  79.8 2.6 %copy.15 = bf16[8,128,768]{2,1,0:T(8,128)(2,1)} copy(bf16[8,128,768]{1,2,0:T(8,128)(2,1)} %bitcast.1) | data formatting | bytes 3145728 | tf_op jit(solution)/shard_map/all_to_all | solution.py:46
  82.4 10.9 %fusion.1 = (f32[3072]{0:T(1024)S(1)}, f32[768]{0:T(1024)S(1)}, f32[3072,768]{1,0:T(8,128)}) fusion(bf16[1024,3072]{1,0:T(8,128)(2,1)} %all-gather.5.cloned.1.call-done, bf16[1024,768]{1,0:T(8,128)(2,1)} %bitcast.29), kind=kOutput, calls=%fused_computation.5 | convolution fusion | flops 4841271296 | bytes 17316864 | tf_op jit(solution)/shard_map/dot_general | solution.py:22
  93.2 11.4 %all-reduce.2 = (f32[]{:T(128)}, f32[768]{0:T(1024)S(1)}) all-reduce(f32[]{:T(128)} %reduce_sum.65, f32[768]{0:T(1024)S(1)} %get-tuple-element.24), channel_id=1, replica_groups=mesh['dp'=8,'mp'=4] {'mp'}, use_global_device_ids=true, to_apply=%region_5.0 | all-reduce | flops 769 | bytes 6152 | tf_op jit(solution)/shard_map/psum | solution.py:63
  104.6 0.7 multiply_add_fusion.5
  105.3 25.0 %all-reduce.1 = (f32[]{:T(128)}, f32[3072]{0:T(1024)S(1)}) all-reduce(f32[]{:T(128)} %get-tuple-element.37, f32[3072]{0:T(1024)S(1)} %get-tuple-element.23), channel_id=1, replica_groups=mesh['dp'=8,'mp'=4] {'dp'}, use_global_device_ids=true, to_apply=%region_7.0 | all-reduce | flops 3073 | bytes 24584 | tf_op jit(solution)/shard_map/psum | solution.py:65
  131.5 11.3 %multiply_subtract_fusion.1 = f32[3072,768]{1,0:T(8,128)} fusion(f32[3072,768]{1,0:T(8,128)} %param.17, f32[3072,768]{1,0:T(8,128)} %get-tuple-element.38, f32[]{:T(128)S(6)} %div.48, f32[768]{0:T(1024)S(1)} %get-tuple-element.36, f32[3072]{0:T(1024)S(1)} %multiply_add_fusion.3), kind=kLoop, calls=%fused_computation.2 | loop fusion | flops 11796480 | bytes 28326916 | tf_op jit(solution)/shard_map/sub | solution.py:69
  142.8 0.0 collective-permute-done.2
  142.8 0.0 collective-permute-done.1
  142.8 0.0 collective-permute-done
  142.8 0.0 all-gather.3.cloned.1.call-done
  142.9 0.0 all-to-all-done.1
  142.9 0.0 copy-start.6
  142.9 0.0 copy-start.4
  142.9 11.3 %fusion.2 = (f32[3072]{0:T(1024)S(1)}, f32[768]{0:T(1024)S(1)}, f32[768,3072]{1,0:T(8,128)}) fusion(bf16[1024,768]{1,0:T(8,128)(2,1)S(1)} %bitcast.28, bf16[1024,3072]{1,0:T(8,128)(2,1)} %all-gather.3.cloned.1.call-done), kind=kOutput, calls=%fused_computation.6 | convolution fusion | flops 4841271296 | bytes 17316864 | tf_op jit(solution)/shard_map/dot_general | solution.py:22
  154.2 8.3 %psum.53 = f32[768]{0:T(1024)S(1)} all-reduce(f32[768]{0:T(1024)S(1)} %get-tuple-element.22), channel_id=1, replica_groups=mesh['dp'=8,'mp'=4] {'mp'}, use_global_device_ids=true, to_apply=%region_9.0 | all-reduce | flops 768 | bytes 6144 | tf_op jit(solution)/shard_map/psum | solution.py:76
  162.5 0.6 fusion.12
  163.1 23.4 %all-reduce = (f32[]{:T(128)}, f32[3072]{0:T(1024)S(1)}) all-reduce(f32[]{:T(128)} %get-tuple-element.31, f32[3072]{0:T(1024)S(1)} %get-tuple-element.21), channel_id=1, replica_groups=mesh['dp'=8,'mp'=4] {'dp'}, use_global_device_ids=true, to_apply=%region_13.0 | all-reduce | flops 3073 | bytes 24584 | tf_op jit(solution)/shard_map/psum | solution.py:78
  187.2 2.0 add_convert_fusion
  189.2 11.7 %multiply_subtract_fusion = f32[768,3072]{1,0:T(8,128)} fusion(f32[768,3072]{1,0:T(8,128)} %param.16, f32[768,3072]{1,0:T(8,128)} %get-tuple-element.39, f32[]{:T(128)S(6)} %div.54, f32[3072]{0:T(1024)S(1)} %multiply_add_fusion.2, f32[768]{0:T(1024)S(1)} %get-tuple-element.32), kind=kLoop, calls=%fused_computation | loop fusion | flops 11796480 | bytes 28326916 | tf_op jit(solution)/shard_map/sub | solution.py:82
  (11 shorter events, 0.0 us)
Async XLA Ops:
  7.2 2.7 %copy-start.2 = (bf16[128,3072]{1,0:T(8,128)(2,1)S(1)}, bf16[128,3072]{1,0:T(8,128)(2,1)}, u32[]{:S(2)}) copy-start(bf16[128,3072]{1,0:T(8,128)(2,1)} %param.12) | copy-start | bytes 2359300
  7.2 2.7 %copy-start.1 = (bf16[128,6144]{1,0:T(8,128)(2,1)S(1)}, bf16[128,6144]{1,0:T(8,128)(2,1)}, u32[]{:S(2)}) copy-start(bf16[128,6144]{1,0:T(8,128)(2,1)} %param.13) | copy-start | bytes 4718596
  7.2 75.2 %all-gather.5.cloned.1.call-start = ((), (), s32[]{:S(2)}) async-start(), calls=%async_computation.3 | async-start | bytes 7077888 | tf_op jit(solution)/shard_map/all_gather | solution.py:44
  9.8 133.1 %all-gather.3.cloned.1.call-start = ((), (), s32[]{:S(2)}) async-start(), calls=%async_computation.2 | async-start | bytes 7077888 | tf_op jit(solution)/shard_map/all_gather | solution.py:51
  31.4 44.6 %all-to-all-start = ((bf16[128,8,768]{0,2,1:T(8,128)(2,1)}), bf16[128,8,768]{0,2,1:T(8,128)(2,1)}, u32[]{:S(2)}, u32[]{:S(2)}) async-start(bf16[128,8,768]{0,2,1:T(8,128)(2,1)} %bitcast), calls=%async_computation | async-start | bytes 3145728 | tf_op jit(solution)/shard_map/all_to_all | solution.py:46
  55.2 6.2 %copy-start.3 = (f32[3072]{0:T(1024)S(1)}, f32[3072]{0:T(1024)}, u32[]{:S(2)}) copy-start(f32[3072]{0:T(1024)} %param.20) | copy-start | bytes 36868
  56.3 86.5 %collective-permute-start.2 = (bf16[128,1536]{1,0:T(8,128)(2,1)}, bf16[128,1536]{1,0:T(8,128)(2,1)S(1)}, u32[]{:S(2)}, u32[]{:S(2)}) collective-permute-start(bf16[128,1536]{1,0:T(8,128)(2,1)} %get-tuple-element.33), channel_id=1, source_target_pairs={{0,3},{1,0},{2,1},{3,2},{4,7},{5,4},{6,5},{7,6},{8,11},{9,8},{10,9... | collective-permute-start | bytes 1179656 | tf_op jit(solution)/shard_map/ppermute | solution.py:35
  60.3 82.5 %collective-permute-start.1 = (bf16[128,1536]{1,0:T(8,128)(2,1)}, bf16[128,1536]{1,0:T(8,128)(2,1)}, u32[]{:S(2)}, u32[]{:S(2)}) collective-permute-start(bf16[128,1536]{1,0:T(8,128)(2,1)} %get-tuple-element.34), channel_id=1, source_target_pairs={{0,2},{1,3},{2,0},{3,1},{4,6},{5,7},{6,4},{7,5},{8,10},{9,11},{10,... | collective-permute-start | bytes 1179656 | tf_op jit(solution)/shard_map/ppermute | solution.py:35
  60.3 82.5 %collective-permute-start = (bf16[128,1536]{1,0:T(8,128)(2,1)}, bf16[128,1536]{1,0:T(8,128)(2,1)}, u32[]{:S(2)}, u32[]{:S(2)}) collective-permute-start(bf16[128,1536]{1,0:T(8,128)(2,1)} %get-tuple-element.35), channel_id=1, source_target_pairs={{0,1},{1,2},{2,3},{3,0},{4,5},{5,6},{6,7},{7,4},{8,9},{9,10},{10,1... | collective-permute-start | bytes 1179656 | tf_op jit(solution)/shard_map/ppermute | solution.py:35
  76.0 66.9 %all-to-all-start.1 = ((bf16[8,128,768]{2,1,0:T(8,128)(2,1)}), bf16[8,128,768]{2,1,0:T(8,128)(2,1)S(1)}, u32[]{:S(2)}, u32[]{:S(2)}) async-start(bf16[8,128,768]{2,1,0:T(8,128)(2,1)} %bitcast_dynamic-update-slice_fusion), calls=%async_computation.1 | async-start | bytes 3145728 | tf_op jit(solution)/shard_map/all_to_all | solution.py:57
  82.4 22.3 %copy-start.5 = (f32[768]{0:T(1024)S(1)}, f32[768]{0:T(1024)}, u32[]{:S(2)}) copy-start(f32[768]{0:T(1024)} %param.21) | copy-start | bytes 9220
  142.9 19.6 %copy-start.6 = (f32[768]{0:T(1024)S(1)}, f32[768]{0:T(1024)}, u32[]{:S(2)}) copy-start(f32[768]{0:T(1024)} %param.18) | copy-start | bytes 9220
  142.9 44.2 %copy-start.4 = (f32[3072]{0:T(1024)S(1)}, f32[3072]{0:T(1024)}, u32[]{:S(2)}) copy-start(f32[3072]{0:T(1024)} %param.19) | copy-start | bytes 36868
  142.9 44.3 %copy-start = (f32[128,1536]{1,0:T(8,128)S(1)}, f32[128,1536]{1,0:T(8,128)}, u32[]{:S(2)}) copy-start(f32[128,1536]{1,0:T(8,128)} %constant_dynamic-slice_fusion) | copy-start | bytes 2359300
Sparse Core Ops, SparseCore 0:
  9.9 64.6 all-gather.4
  76.5 57.3 all-gather.2
